TPU v7x, 256 devices: a whole 4x4x8 slice. The times are simulated.
256 devices in a mesh: gx: 8 (over y, core), gy: 4 (over z_lo), gz: 8 (over x, z_hi).
Axes of the slice: x: 4, y: 4, z: 8 (z_hi: 2, z_lo: 4; z = z_hi * 4 + z_lo), core: 2. Of those that a mesh axis runs over, the one named last changes fastest.
Arguments:
- stream: bfloat16 [65536, 8192], P(('gx', 'gy', 'gz')), may hold values from -4 to 4
- segment_ids: int32 [65536], P(('gx', 'gy', 'gz')), may hold values from 0 to 65535, as said below
- positions: int32 [65536], P(('gx', 'gy', 'gz')), may hold values from 0 to 255, as said below
- norm_gain: bfloat16 [1, 8192], P(None, ('gx', 'gy', 'gz')), may hold values from 0.099609375 to 1.8984375
- q_weight: bfloat16 [1, 8192, 512], P(None, ('gx', 'gy', 'gz')), as said below
- k_weight: bfloat16 [1, 8192, 128], P(None, ('gx', 'gy', 'gz')), as said below
- v_weight: bfloat16 [1, 8192, 128], P(None, ('gx', 'gy', 'gz')), may hold values from -0.0625 to 0.0625
- o_weight: bfloat16 [1, 512, 8192], P(None, None, ('gx', 'gy', 'gz')), may hold values from -0.25 to 0.25
Outputs:
- result: bfloat16 [65536, 8192], P(('gx', 'gy', 'gz'))
Inputs may be any that keep to these rules, and one draw needn't show every extreme that they name: `segment_ids`: each token's id is the index of its document's first token, so ids never fall along the tokens; every document lies inside one aligned block of 256 tokens, every block starts a new document, and the last token is a document of its own. `positions`: counts from 0 at a document's first token and rises by one per token. `q_weight`: A projection scaled by its fan-in. `k_weight`: A projection scaled by its fan-in.
All inputs are finite; a program needn't handle non-finite values.
Results may differ from a plain program's by a relative error of at most 0.0064.
Values may be sent and summed in bfloat16 or wider, within the bound.
No kernel may reach another device: no remote copies, remote signals or barrier semaphores. Data moves between devices by JAX's collectives and lax.ppermute only.
A program may use at most 128 MiB of HBM per device.

v0:
```python
import functools
import math

import jax
import jax.numpy as jnp
from jax import lax
from jax.experimental import pallas as pl
from jax.experimental.pallas import tpu as pltpu
from jax.sharding import Mesh, PartitionSpec as P


AXES = ("y", "c", "zl", "x", "zh")
NY, NC, NZL, NX, NZH = 4, 2, 4, 4, 2
RING = {"x": (("c", "x"), 4), "y": (("y", "c"), 4), "z": (("c", "zl", "zh"), 8)}
HD = 128
ROWS = 32
T = 256


def position(axis):
    if axis == "z":
        return lax.axis_index("zh") * NZL + lax.axis_index("zl")
    return lax.axis_index(axis)


def exchange(block, axis, step):
    names, n = RING[axis]

    def number(p, c):
        if axis == "z":
            return (c * NZL + p % NZL) * NZH + p // NZL
        return c * n + p if axis == "x" else p * NC + c

    pairs = []
    for p in range(n):
        for c in range(NC):
            right = ((p + c) % 2 == 0) == (step % 2 == 0)
            pairs.append((number(p, c), number((p + (1 if right else -1)) % n, c)))
    return lax.ppermute(block, names, pairs)


def gather(block, axis):
    n = RING[axis][1]
    other = exchange(block, axis, 0)
    first = (position(axis) + lax.axis_index("c")) % 2 == 0
    current = jnp.where(first, jnp.stack([block, other]), jnp.stack([other, block]))
    found = [current]
    for step in range(1, n // 2):
        current = exchange(current, axis, step)
        found.append(current)
    return found


def slots(axis, core):
    n = RING[axis][1]
    k = lax.iota(jnp.int32, n)
    p = position(axis)
    left = (p + core) & 1
    off = jnp.where((k >> 1) & 1 == 1, -((k >> 1) + 1), k >> 1 & -2)
    return (p - left + (1 - 2 * left) * off + (k & 1)) & (n - 1)


def near(axis, core):
    k = lax.iota(jnp.int32, 4)
    p = position(axis)
    turn = 1 - 2 * ((p + core) & 1)
    return (p + turn * jnp.where(k == 2, -1, k) + jnp.where(k == 3, -turn, 0)) & 3


def spread(block, axis):
    one = exchange(block, axis, 0)
    two = exchange(block, axis, 1)
    return [block, one, two, exchange(one, axis, 1)]


Z, ZP, X, Y, XO, YO, CORE = 0, 8, 16, 20, 24, 28, 32


def table():
    core = lax.axis_index("c")
    parts = [slots("z", core), slots("z", 1 - core), near("x", core), near("y", core)]
    parts += [slots("x", core), slots("y", core), core[None]]
    return jnp.concatenate(parts).astype(jnp.int32)


def arrange_columns_kernel(tab, p0, p1, p2, p3, a_ref, b_ref):
    for n, p in enumerate((p0, p1, p2, p3)):
        for i in range(2):
            z = tab[Z + n * 2 + i]
            a_ref[z % NZL, z // NZL] = p[i, :, :384]
            b_ref[z % NZL, z // NZL] = p[i, :, 384:]


def arrange_kernel(at, tab, p0, p1, p2, p3, out_ref):
    for n, p in enumerate((p0, p1, p2, p3)):
        out_ref[tab[at + n]] = p[...]


def arrange_plane_kernel(tab, p0, p1, out_ref):
    for n, p in enumerate((p0, p1)):
        for i in range(2):
            for j in range(4):
                out_ref[tab[YO + n * 2 + i], tab[XO + j]] = p[i, j]


def local(kernel, tab, arrays, shapes):
    vmem = pl.BlockSpec(memory_space=pltpu.VMEM)
    out = [jax.ShapeDtypeStruct(s, jnp.bfloat16) for s in shapes]
    return pl.pallas_call(
        kernel,
        in_specs=[pl.BlockSpec(memory_space=pltpu.SMEM)] + [vmem] * len(arrays),
        out_specs=[vmem] * len(out),
        out_shape=out,
    )(tab, *arrays)


def rope(h, cos, sin):
    return h * cos + pltpu.roll(h, HD // 2, 1) * sin


def other_half_kernel(tab, x_ref, out_ref, sem):
    copies = [
        pltpu.make_async_copy(
            x_ref.at[:, pl.ds(y * 2048 + (1 - tab[CORE]) * 1024, 1024)],
            out_ref.at[:, pl.ds(y * 1024, 1024)],
            sem.at[y],
        )
        for y in range(NY)
    ]
    for c in copies:
        c.start()
    for c in copies:
        c.wait()


def token_copies(tab, x_ref, xp_ref, y, dst, sems):
    return [
        pltpu.make_async_copy(
            x_ref.at[:, pl.ds(pl.multiple_of(y * 2048 + tab[CORE] * 1024, 1024), 1024)], dst.at[pl.ds(0, T)], sems[0]
        ),
        pltpu.make_async_copy(
            xp_ref.at[:, pl.ds(pl.multiple_of(y * 1024, 1024), 1024)], dst.at[pl.ds(T, T)], sems[1]
        ),
    ]


def prepare_kernel(tab, x_ref, xp_ref, xb_ref, ps, sem):
    copies = [token_copies(tab, x_ref, xp_ref, y, ps.at[y], (sem.at[y], sem.at[4 + y])) for y in range(NY)]
    for pair in copies:
        for c in pair:
            c.start()
    low = lax.broadcasted_iota(jnp.int32, (2 * T, 128), 1) < 64
    for y in range(NY):
        for c in copies[y]:
            c.wait()
        for zl in range(0, NZL, 2):
            for x in range(NX):
                at = zl * 256 + x // 2 * 128
                one = ps[y, :, at : at + 128].astype(jnp.float32)
                two = ps[y, :, at + 256 : at + 384].astype(jnp.float32)
                if x % 2 == 0:
                    both = jnp.where(low, one, pltpu.roll(two, 64, 1))
                else:
                    both = jnp.where(low, pltpu.roll(one, 64, 1), two)
                xb_ref[x, :, y * 256 + zl * 64 : y * 256 + zl * 64 + 128] = both.astype(jnp.bfloat16)


def product(colour, slot, count, tab, x_refs, w_refs, x, w, sem):
    x_ref, xp_ref, xb_ref = x_refs
    waits = []
    for i in range(count):
        if colour == "a":
            group = token_copies(tab, x_ref, xp_ref, tab[Y + slot + i], x.at[i], (sem.at[3 * i], sem.at[3 * i + 1]))
            blocks = [pltpu.make_async_copy(w_refs[i].at[j], w.at[i, :, j], sem.at[3 * i + 2]) for j in range(NX)]
        else:
            group = [pltpu.make_async_copy(xb_ref.at[tab[X + slot + i]], x.at[i], sem.at[3 * i])]
            blocks = [pltpu.make_async_copy(w_refs[i], w.at[i], sem.at[3 * i + 2])]
        for c in group + blocks:
            c.start()
        waits.append(group + [pltpu.make_async_copy(w.at[i], w.at[i], sem.at[3 * i + 2])])

    def finish():
        total = None
        for i in range(count):
            for c in waits[i]:
                c.wait()
            part = jnp.dot(x[i], w[i].reshape(1024, 384), preferred_element_type=jnp.float32)
            total = part if total is None else total + part
        return total

    return finish


def first_kernel(colour, tab, x_ref, xp_ref, xb_ref, w0, w1, w2, out_ref, x, w, sem):
    out_ref[...] = product(colour, 0, 3, tab, (x_ref, xp_ref, xb_ref), (w0, w1, w2), x, w, sem)()


def last_kernel(tab, x_ref, xp_ref, xb_ref, a, b, ta_ref, tb_ref, own_ref, par_ref, x, wa, wb, t, sem, tsem):
    x_refs = (x_ref, xp_ref, xb_ref)
    finish = [product("a", 3, 1, tab, x_refs, (a,), x.at[pl.ds(0, 1)], wa, sem.at[pl.ds(0, 3)])]
    finish.append(product("b", 3, 1, tab, x_refs, (b,), x.at[pl.ds(1, 1)], wb, sem.at[pl.ds(3, 3)]))
    before = [pltpu.make_async_copy(r, t.at[n], tsem.at[n]) for n, r in enumerate((ta_ref, tb_ref))]
    for c in before:
        c.start()
    for n in range(2):
        total = finish[n]()
        before[n].wait()
        total += t[n]
        own_ref[:, n * 384 : n * 384 + 384] = total[:T]
        par_ref[:, n * 384 : n * 384 + 384] = total[T:]


WEIGHTS = {"a": (NZL, NX, NZH, ROWS, 384), "b": (NY, NZL, NZH, ROWS, 384)}


def first_products(colour, tab, xs, w):
    hbm = pl.BlockSpec(memory_space=pl.ANY)
    return pl.pallas_call(
        functools.partial(first_kernel, colour),
        in_specs=[pl.BlockSpec(memory_space=pltpu.SMEM)] + [hbm] * 6,
        out_specs=pl.BlockSpec(memory_space=pltpu.VMEM),
        out_shape=jax.ShapeDtypeStruct((2 * T, 384), jnp.float32),
        scratch_shapes=[
            pltpu.VMEM((3, 2 * T, 1024), jnp.bfloat16),
            pltpu.VMEM((3, *WEIGHTS[colour]), jnp.bfloat16),
            pltpu.SemaphoreType.DMA((9,)),
        ],
    )(tab, *xs, *w)


def last_products(tab, xs, a, b, ta, tb):
    hbm = pl.BlockSpec(memory_space=pl.ANY)
    return pl.pallas_call(
        last_kernel,
        in_specs=[pl.BlockSpec(memory_space=pltpu.SMEM)] + [hbm] * 7,
        out_specs=[pl.BlockSpec(memory_space=pltpu.VMEM)] * 2,
        out_shape=[jax.ShapeDtypeStruct((T, 768), jnp.float32)] * 2,
        scratch_shapes=[
            pltpu.VMEM((2, 2 * T, 1024), jnp.bfloat16),
            pltpu.VMEM((1, *WEIGHTS["a"]), jnp.bfloat16),
            pltpu.VMEM((1, *WEIGHTS["b"]), jnp.bfloat16),
            pltpu.VMEM((2, 2 * T, 384), jnp.float32),
            pltpu.SemaphoreType.DMA((6,)),
            pltpu.SemaphoreType.DMA((2,)),
        ],
        name="last",
    )(tab, *xs, a, b, ta, tb)


def finish_kernel(
    tab, own_ref, par_ref, inv_ref, cos_ref, sin_ref, mask_ref, x_ref,
    o0, o1, o2, o3, p0, p1, p2, p3, out_ref, ot, xs, ys, mixed, sem, ysem,
):
    pltpu.make_async_copy(x_ref, xs, sem.at[0]).start()
    core = tab[CORE]
    for at, pieces, c in ((Z, (o0, o1, o2, o3), core), (ZP, (p0, p1, p2, p3), 1 - core)):
        for n, piece in enumerate(pieces):
            for i in range(2):
                z = tab[at + n * 2 + i]
                for y in range(NY):
                    pltpu.make_async_copy(
                        piece.at[i, y], ot.at[y, c, z % NZL, :, z // NZL], sem.at[1]
                    ).start()
    inv, cos, sin = inv_ref[...], cos_ref[...], sin_ref[...]
    allowed = mask_ref[...] > 0

    def raw(col):
        return (own_ref[:, col : col + HD] + par_ref[:, col : col + HD]) * inv

    keys = rope(raw(512), cos, sin).astype(jnp.bfloat16)
    values = raw(640).astype(jnp.bfloat16)
    for h in range(4):
        q = rope(raw(h * HD), cos, sin).astype(jnp.bfloat16)
        s = lax.dot_general(q, keys, (((1,), (1,)), ((), ())), preferred_element_type=jnp.float32)
        s = jnp.where(allowed, s * (1.0 / math.sqrt(HD)), -1e30)
        e = jnp.exp(s - jnp.max(s, -1, keepdims=True))
        probs = (e / jnp.sum(e, -1, keepdims=True)).astype(jnp.bfloat16)
        mixed[:, h * HD : h * HD + HD] = jnp.dot(
            probs, values, preferred_element_type=jnp.float32
        ).astype(jnp.bfloat16)
    pltpu.make_async_copy(xs, xs, sem.at[0]).wait()
    pltpu.make_async_copy(ot, ot, sem.at[1]).wait()
    writes = []
    for k in range(NY * NC):
        rows = ot[k // NC, k % NC].reshape(1024, 512)
        branch = lax.dot_general(
            mixed[...], rows, (((1,), (1,)), ((), ())), preferred_element_type=jnp.float32
        )
        ys[k] = (xs[:, k * 1024 : k * 1024 + 1024].astype(jnp.float32) + branch).astype(jnp.bfloat16)
        writes.append(pltpu.make_async_copy(ys.at[k], out_ref.at[:, pl.ds(k * 1024, 1024)], ysem.at[k]))
        writes[-1].start()
    for w in writes:
        w.wait()


def body(stream, segment_ids, positions, norm_gain, q_weight, k_weight, v_weight, o_weight):
    gain = norm_gain[0].astype(jnp.float32)[:, None]
    qkv = jnp.concatenate([q_weight[0], k_weight[0], v_weight[0]], -1)
    qkv = lax.optimization_barrier((qkv.astype(jnp.float32) * gain).astype(jnp.bfloat16))

    tab = table()
    smem = pl.BlockSpec(memory_space=pltpu.SMEM)
    vmem = pl.BlockSpec(memory_space=pltpu.VMEM)
    hbm = pl.BlockSpec(memory_space=pl.ANY)

    shape = (NZL, NZH, ROWS, 384)
    a, b = local(arrange_columns_kernel, tab, gather(qkv, "z"), [shape] * 2)
    a, b = spread(a, "x"), spread(b, "y")
    (a,) = local(functools.partial(arrange_kernel, X), tab, a, [(NX, *shape)])
    (b,) = local(functools.partial(arrange_kernel, Y), tab, b, [(NY, *shape)])
    a, b = spread(a, "y"), spread(b, "x")

    o, _ = lax.optimization_barrier((o_weight[0].T, qkv))
    o = jnp.concatenate(gather(o, "x"))
    (o,) = local(arrange_plane_kernel, tab, gather(o, "y"), [(NY, NX, ROWS, 512)])
    o = gather(o, "z")

    def swap(a):
        return lax.ppermute(a, "c", [(0, 1), (1, 0)])

    o_par = [swap(v) for v in o]

    freqs = jnp.exp(-math.log(500000.0) * jnp.arange(HD // 2, dtype=jnp.float32) * 2.0 / HD)
    angles = positions.astype(jnp.float32)[:, None] * freqs[None, :]
    cos, sin = jnp.cos(angles), jnp.sin(angles)
    cos = jnp.concatenate([cos, cos], -1)
    sin = jnp.concatenate([-sin, sin], -1)
    allowed = (segment_ids[:, None] == segment_ids[None, :]) & (positions[None, :] <= positions[:, None])
    mask = allowed.astype(jnp.float32)

    x_par = pl.pallas_call(
        other_half_kernel,
        in_specs=[smem, hbm],
        out_specs=vmem,
        out_shape=jax.ShapeDtypeStruct((T, 4096), jnp.bfloat16),
        scratch_shapes=[pltpu.SemaphoreType.DMA((NY,))],
        name="other_half",
    )(tab, stream)
    x_par = swap(x_par)
    x_cut = pl.pallas_call(
        prepare_kernel,
        in_specs=[smem, hbm, hbm],
        out_specs=vmem,
        out_shape=jax.ShapeDtypeStruct((4, 2 * T, 1024), jnp.bfloat16),
        scratch_shapes=[
            pltpu.VMEM((4, 2 * T, 1024), jnp.bfloat16),
            pltpu.SemaphoreType.DMA((8,)),
        ],
        name="prepare",
    )(tab, stream, x_par)
    wide = stream.astype(jnp.float32)
    inv = lax.rsqrt(jnp.mean(wide * wide, -1, keepdims=True) + 1e-05)
    xs = (stream, x_par, x_cut)
    total_a = first_products("a", tab, xs, a[:3])
    total_b = first_products("b", tab, xs, b[:3])
    own, par = last_products(tab, xs, a[3], b[3], total_a, total_b)
    par = swap(par)
    return pl.pallas_call(
        finish_kernel,
        in_specs=[smem] + [vmem] * 6 + [hbm] * 9,
        out_specs=hbm,
        out_shape=jax.ShapeDtypeStruct((T, 8192), jnp.bfloat16),
        scratch_shapes=[
            pltpu.VMEM((NY, NC, NZL, NX, NZH, ROWS, 512), jnp.bfloat16),
            pltpu.VMEM((T, 8192), jnp.bfloat16),
            pltpu.VMEM((NY * NC, T, 1024), jnp.bfloat16),
            pltpu.VMEM((T, 512), jnp.bfloat16),
            pltpu.SemaphoreType.DMA((2,)),
            pltpu.SemaphoreType.DMA((NY * NC,)),
        ],
        name="finish",
    )(tab, own, par, inv, cos, sin, mask, stream, *o, *o_par)


def solution(mesh):
    fine = Mesh(mesh.devices.reshape(NY, NC, NZL, NX, NZH), AXES)
    in_specs = (
        P(AXES, None),
        P(AXES),
        P(AXES),
        P(None, AXES),
        P(None, AXES, None),
        P(None, AXES, None),
        P(None, AXES, None),
        P(None, None, AXES),
    )

    return jax.shard_map(body, mesh=fine, in_specs=in_specs, out_specs=P(AXES, None), check_vma=False)
```

profile of v0, /device:TPU:1, one launch (start us, length us, event | category | flops | bytes accessed | tf_op | source)
XLA Modules:
  0.0 180.4 jit_solution(12070813497825959124)
XLA Ops:
  1.5 3.3 %collective-permute-start.18 = (bf16[32,512]{1,0:T(8,128)(2,1)}, bf16[32,512]{1,0:T(8,128)(2,1)S(1)}, u32[]{:S(2)}, u32[]{:S(2)}) collective-permute-start(bf16[32,512]{1,0:T(8,128)(2,1)} %bitcast.26), channel_id=1, source_target_pairs={{0,2},{32,38},{2,0},{34,36},{4,6},{36,34},{6,4},{38,32},{1,3},{33,... | collective-permute-start | bytes 98312 | tf_op jit(solution)/shard_map/ppermute | solution.py:39
  7.5 2.9 %collective-permute-done.19 = bf16[2,32,512]{2,1,0:T(8,128)(2,1)S(1)} collective-permute-done((bf16[2,32,512]{2,1,0:T(8,128)(2,1)S(1)}, bf16[2,32,512]{2,1,0:T(8,128)(2,1)S(1)}, u32[]{:S(2)}, u32[]{:S(2)}) %collective-permute-start.19) | collective-permute-done | bytes 65568 | tf_op jit(solution)/shard_map/ppermute | solution.py:39
  10.5 3.0 %collective-permute-start.20 = (bf16[4,32,512]{2,1,0:T(8,128)(2,1)S(1)}, bf16[4,32,512]{2,1,0:T(8,128)(2,1)S(1)}, u32[]{:S(2)}, u32[]{:S(2)}) collective-permute-start(bf16[4,32,512]{2,1,0:T(8,128)(2,1)S(1)} %get-tuple-element.16), channel_id=1, source_target_pairs={{0,64},{32,224},{64,0},{96,160},{128,192},{160,96},{192,128},{224,... | collective-permute-start | bytes 393224 | tf_op jit(solution)/shard_map/ppermute | solution.py:39
  16.7 5.8 %collective-permute-done.21.p1 = bf16[2,4,32,512]{3,2,1,0:T(8,128)(2,1)S(1)} collective-permute-done((bf16[2,4,32,512]{3,2,1,0:T(8,128)(2,1)S(1)}, bf16[2,4,32,512]{3,2,1,0:T(8,128)(2,1)S(1)}, u32[]{:S(2)}, u32[]{:S(2)}) %collective-permute-start.21) | collective-permute-done | bytes 262176 | tf_op jit(solution)/shard_map/ppermute | solution.py:39
  25.1 4.2 %collective-permute-start.22 = (bf16[4,4,32,512]{3,2,1,0:T(8,128)(2,1)}, bf16[4,4,32,512]{3,2,1,0:T(8,128)(2,1)S(1)}, u32[]{:S(2)}, u32[]{:S(2)}) collective-permute-start(bf16[4,4,32,512]{3,2,1,0:T(8,128)(2,1)} %shard_map.87), channel_id=1, source_target_pairs={{0,8},{32,57},{8,0},{40,48},{16,24},{48,40},{24,16},{56,33},{1,9},... | collective-permute-start | bytes 1572872 | tf_op jit(solution)/shard_map/ppermute | solution.py:39
  29.3 6.8 %collective-permute-done.22 = bf16[4,4,32,512]{3,2,1,0:T(8,128)(2,1)S(1)} collective-permute-done((bf16[4,4,32,512]{3,2,1,0:T(8,128)(2,1)}, bf16[4,4,32,512]{3,2,1,0:T(8,128)(2,1)S(1)}, u32[]{:S(2)}, u32[]{:S(2)}) %collective-permute-start.22) | collective-permute-done | bytes 524320 | tf_op jit(solution)/shard_map/ppermute | solution.py:39
  37.6 2.8 %collective-permute-start.1 = (bf16[32,768]{1,0:T(8,128)(2,1)S(1)}, bf16[32,768]{1,0:T(8,128)(2,1)S(1)}, u32[]{:S(2)}, u32[]{:S(2)}) collective-permute-start(bf16[32,768]{1,0:T(8,128)(2,1)S(1)} %multiply_convert_fusion), channel_id=1, source_target_pairs={{0,8},{32,57},{8,0},{40,48},{16,24},{48,40},{24,16},{56,33},{1,9},... | collective-permute-start | bytes 147464 | tf_op jit(solution)/shard_map/ppermute | solution.py:39
  42.1 11.8 %collective-permute-done.2.p1 = bf16[2,32,768]{2,1,0:T(8,128)(2,1)S(1)} collective-permute-done((bf16[2,32,768]{2,1,0:T(8,128)(2,1)S(1)}, bf16[2,32,768]{2,1,0:T(8,128)(2,1)S(1)}, u32[]{:S(2)}, u32[]{:S(2)}) %collective-permute-start.2) | collective-permute-done | bytes 98336 | tf_op jit(solution)/shard_map/ppermute | solution.py:39
  56.5 3.5 %other_half.1 = bf16[256,4096]{1,0:T(8,128)(2,1)} custom-call(s32[33]{0:T(128)} %concatenate.15.tab, bf16[256,8192]{1,0:T(8,128)(2,1)} %x_ref.11), custom_call_target="tpu_custom_call" | custom-call | tf_op jit(solution)/shard_map/other_half/pallas_call | solution.py:331
  60.0 5.3 %collective-permute-start = (bf16[256,4096]{1,0:T(8,128)(2,1)}, bf16[256,4096]{1,0:T(8,128)(2,1)S(1)}, u32[]{:S(2)}, u32[]{:S(2)}) collective-permute-start(bf16[256,4096]{1,0:T(8,128)(2,1)} %other_half.1), channel_id=1, source_target_pairs={{0,32},{32,0},{1,33},{33,1},{2,34},{34,2},{3,35},{35,3},{4,36},{36... | collective-permute-start | bytes 6291464 | tf_op jit(solution)/shard_map/ppermute | solution.py:319
  65.3 2.9 %collective-permute-start.24 = (bf16[2,4,4,32,512]{4,3,2,1,0:T(8,128)(2,1)}, bf16[2,4,4,32,512]{4,3,2,1,0:T(8,128)(2,1)}, u32[]{:S(2)}, u32[]{:S(2)}) collective-permute-start(bf16[2,4,4,32,512]{4,3,2,1,0:T(8,128)(2,1)} %collective-permute-done.23.o1), channel_id=1, source_target_pairs={{0,8},{32,57},{8,0},{40,48},{16,24},{48,40},{24,16},{56,33},{1,9},... | collective-permute-start | bytes 3145736 | tf_op jit(solution)/shard_map/ppermute | solution.py:39
  68.3 4.9 %collective-permute-done.4.p3 = bf16[2,32,768]{2,1,0:T(8,128)(2,1)S(1)} collective-permute-done((bf16[2,32,768]{2,1,0:T(8,128)(2,1)S(1)}, bf16[2,32,768]{2,1,0:T(8,128)(2,1)S(1)}, u32[]{:S(2)}, u32[]{:S(2)}) %collective-permute-start.4) | collective-permute-done | bytes 98336 | tf_op jit(solution)/shard_map/ppermute | solution.py:39
  75.7 2.8 %collective-permute-start.10 = (bf16[4,2,32,384]{3,2,1,0:T(8,128)(2,1)}, bf16[4,2,32,384]{3,2,1,0:T(8,128)(2,1)S(1)}, u32[]{:S(2)}, u32[]{:S(2)}) collective-permute-start(bf16[4,2,32,384]{3,2,1,0:T(8,128)(2,1)} %get-tuple-element.11.p0), channel_id=1, source_target_pairs={{0,64},{32,224},{64,0},{96,160},{128,192},{160,96},{192,128},{224,... | collective-permute-start | bytes 589832 | tf_op jit(solution)/shard_map/ppermute | solution.py:39
  78.5 3.9 %collective-permute-done.10.p1 = bf16[4,2,32,384]{3,2,1,0:T(8,128)(2,1)S(1)} collective-permute-done((bf16[4,2,32,384]{3,2,1,0:T(8,128)(2,1)}, bf16[4,2,32,384]{3,2,1,0:T(8,128)(2,1)S(1)}, u32[]{:S(2)}, u32[]{:S(2)}) %collective-permute-start.10) | collective-permute-done | bytes 196640 | tf_op jit(solution)/shard_map/ppermute | solution.py:39
  93.2 20.2 %collective-permute-done.7.p3 = bf16[4,2,32,384]{3,2,1,0:T(8,128)(2,1)} collective-permute-done((bf16[4,2,32,384]{3,2,1,0:T(8,128)(2,1)S(1)}, bf16[4,2,32,384]{3,2,1,0:T(8,128)(2,1)}, u32[]{:S(2)}, u32[]{:S(2)}) %collective-permute-start.7) | collective-permute-done | bytes 196640 | tf_op jit(solution)/shard_map/ppermute | solution.py:39
  115.6 3.6 %collective-permute-start.8 = (bf16[4,4,2,32,384]{4,3,2,1,0:T(8,128)(2,1)}, bf16[4,4,2,32,384]{4,3,2,1,0:T(8,128)(2,1)}, u32[]{:S(2)}, u32[]{:S(2)}) collective-permute-start(bf16[4,4,2,32,384]{4,3,2,1,0:T(8,128)(2,1)} %shard_map.83.w0), channel_id=1, source_target_pairs={{0,64},{32,224},{64,0},{96,160},{128,192},{160,96},{192,128},{224,... | collective-permute-start | bytes 2359304 | tf_op jit(solution)/shard_map/ppermute | solution.py:39
  119.4 16.3 %collective-permute-done.8.w1 = bf16[4,4,2,32,384]{4,3,2,1,0:T(8,128)(2,1)} collective-permute-done((bf16[4,4,2,32,384]{4,3,2,1,0:T(8,128)(2,1)}, bf16[4,4,2,32,384]{4,3,2,1,0:T(8,128)(2,1)}, u32[]{:S(2)}, u32[]{:S(2)}) %collective-permute-start.8) | collective-permute-done | bytes 786464 | tf_op jit(solution)/shard_map/ppermute | solution.py:39
  135.9 3.5 %collective-permute-start.26 = (bf16[2,4,4,32,512]{4,3,2,1,0:T(8,128)(2,1)S(1)}, bf16[2,4,4,32,512]{4,3,2,1,0:T(8,128)(2,1)}, u32[]{:S(2)}, u32[]{:S(2)}) collective-permute-start(bf16[2,4,4,32,512]{4,3,2,1,0:T(8,128)(2,1)S(1)} %maximum_select_fusion.o0), channel_id=1, source_target_pairs={{0,32},{32,0},{1,33},{33,1},{2,34},{34,2},{3,35},{35,3},{4,36},{36... | collective-permute-start | bytes 3145736 | tf_op jit(solution)/shard_map/ppermute | solution.py:319
  140.7 3.1 %multiply_reduce_fusion = f32[256]{0:T(256)S(1)} fusion(bf16[256,8192]{1,0:T(8,128)(2,1)} %x_ref.11), kind=kLoop, calls=%fused_computation | loop fusion | flops 6291200 | bytes 4195328 | tf_op jit(solution)/shard_map/reduce_sum | solution.py:352
  143.8 5.9 %prepare.1.xb_ref = bf16[4,512,1024]{2,1,0:T(8,128)(2,1)} custom-call(s32[33]{0:T(128)} %concatenate.15.tab, bf16[256,8192]{1,0:T(8,128)(2,1)} %x_ref.11, bf16[256,4096]{1,0:T(8,128)(2,1)} %copy-done), custom_call_target="tpu_custom_call" | custom-call | tf_op jit(solution)/shard_map/prepare/pallas_call | solution.py:340
  149.7 5.5 %shard_map.86.tb_ref = f32[512,384]{1,0:T(8,128)} custom-call(s32[33]{0:T(128)} %concatenate.15.tab, bf16[256,8192]{1,0:T(8,128)(2,1)} %x_ref.11, bf16[256,4096]{1,0:T(8,128)(2,1)} %copy-done, bf16[4,512,1024]{2,1,0:T(8,128)(2,1)} %prepare.1.xb_ref, bf16[4,4,2,32,384]{4,3,2,1,0:T(8,128)(2,1)} %shard_map.84.w0, ...), custom_call_target="tpu_custom_call" | custom-call | tf_op jit(solution)/shard_map/pallas_call | solution.py:218
  155.2 5.5 %shard_map.85.ta_ref = f32[512,384]{1,0:T(8,128)} custom-call(s32[33]{0:T(128)} %concatenate.15.tab, bf16[256,8192]{1,0:T(8,128)(2,1)} %x_ref.11, bf16[256,4096]{1,0:T(8,128)(2,1)} %copy-done, bf16[4,512,1024]{2,1,0:T(8,128)(2,1)} %prepare.1.xb_ref, bf16[4,4,2,32,384]{4,3,2,1,0:T(8,128)(2,1)} %shard_map.83.w0, ...), custom_call_target="tpu_custom_call" | custom-call | tf_op jit(solution)/shard_map/pallas_call | solution.py:218
  160.7 5.4 %last.1 = (f32[256,768]{1,0:T(8,128)}, f32[256,768]{1,0:T(8,128)}) custom-call(s32[33]{0:T(128)} %concatenate.15.tab, bf16[256,8192]{1,0:T(8,128)(2,1)} %x_ref.11, bf16[256,4096]{1,0:T(8,128)(2,1)} %copy-done, bf16[4,512,1024]{2,1,0:T(8,128)(2,1)} %prepare.1.xb_ref, bf16[4,4,2,32,384]{4,3,2,1,0:T(8,128)(2,1)} %collective-permute-done.9.a, ...), custom_call_target="tpu_custom_call" | custom-call | tf_op jit(solution)/shard_map/last/pallas_call | solution.py:233
  170.6 9.6 %finish.1 = bf16[256,8192]{1,0:T(8,128)(2,1)} custom-call(s32[33]{0:T(128)} %concatenate.15.tab, f32[256,768]{1,0:T(8,128)} %get-tuple-element.12.own_ref, f32[256,768]{1,0:T(8,128)} %copy-done.3, f32[256,1]{1,0:T(8,128)} %copy.9.inv_ref, f32[256,128]{1,0:T(8,128)} %get-tuple-element.26.cos_ref, f32[256,128]{1,0:T(8,128)} %get-tuple-element.27.sin_ref, ...), custom_call_target="tpu_custom_call" | custom-call | tf_op jit(solution)/shard_map/finish/pallas_call | solution.py:358
  (97 shorter events, 37.3 us)
Async XLA Ops:
  10.5 5.4 %collective-permute-start.20 = (bf16[4,32,512]{2,1,0:T(8,128)(2,1)S(1)}, bf16[4,32,512]{2,1,0:T(8,128)(2,1)S(1)}, u32[]{:S(2)}, u32[]{:S(2)}) collective-permute-start(bf16[4,32,512]{2,1,0:T(8,128)(2,1)S(1)} %get-tuple-element.16), channel_id=1, source_target_pairs={{0,64},{32,224},{64,0},{96,160},{128,192},{160,96},{192,128},{224,... | collective-permute-start | bytes 393224 | tf_op jit(solution)/shard_map/ppermute | solution.py:39
  15.9 6.6 %collective-permute-start.21 = (bf16[2,4,32,512]{3,2,1,0:T(8,128)(2,1)S(1)}, bf16[2,4,32,512]{3,2,1,0:T(8,128)(2,1)S(1)}, u32[]{:S(2)}, u32[]{:S(2)}) collective-permute-start(bf16[2,4,32,512]{3,2,1,0:T(8,128)(2,1)S(1)} %maximum_select_fusion.1.p0), channel_id=1, source_target_pairs={{0,192},{32,96},{64,128},{96,32},{128,64},{160,224},{192,0},{224,1... | collective-permute-start | bytes 786440 | tf_op jit(solution)/shard_map/ppermute | solution.py:39
  25.1 11.0 %collective-permute-start.22 = (bf16[4,4,32,512]{3,2,1,0:T(8,128)(2,1)}, bf16[4,4,32,512]{3,2,1,0:T(8,128)(2,1)S(1)}, u32[]{:S(2)}, u32[]{:S(2)}) collective-permute-start(bf16[4,4,32,512]{3,2,1,0:T(8,128)(2,1)} %shard_map.87), channel_id=1, source_target_pairs={{0,8},{32,57},{8,0},{40,48},{16,24},{48,40},{24,16},{56,33},{1,9},... | collective-permute-start | bytes 1572872 | tf_op jit(solution)/shard_map/ppermute | solution.py:39
  37.5 27.8 %collective-permute-start.23 = (bf16[2,4,4,32,512]{4,3,2,1,0:T(8,128)(2,1)S(1)}, bf16[2,4,4,32,512]{4,3,2,1,0:T(8,128)(2,1)}, u32[]{:S(2)}, u32[]{:S(2)}) collective-permute-start(bf16[2,4,4,32,512]{4,3,2,1,0:T(8,128)(2,1)S(1)} %maximum_select_fusion.o0), channel_id=1, source_target_pairs={{0,25},{32,40},{8,16},{40,32},{16,8},{48,56},{24,1},{56,48},{1,24}... | collective-permute-start | bytes 3145736 | tf_op jit(solution)/shard_map/ppermute | solution.py:39
  41.9 12.0 %collective-permute-start.2 = (bf16[2,32,768]{2,1,0:T(8,128)(2,1)S(1)}, bf16[2,32,768]{2,1,0:T(8,128)(2,1)S(1)}, u32[]{:S(2)}, u32[]{:S(2)}) collective-permute-start(bf16[2,32,768]{2,1,0:T(8,128)(2,1)S(1)} %maximum_select_fusion.2.p0), channel_id=1, source_target_pairs={{0,25},{32,40},{8,16},{40,32},{16,8},{48,56},{24,1},{56,48},{1,24}... | collective-permute-start | bytes 294920 | tf_op jit(solution)/shard_map/ppermute | solution.py:39
  53.9 14.3 %collective-permute-start.3 = (bf16[2,32,768]{2,1,0:T(8,128)(2,1)S(1)}, bf16[2,32,768]{2,1,0:T(8,128)(2,1)S(1)}, u32[]{:S(2)}, u32[]{:S(2)}) collective-permute-start(bf16[2,32,768]{2,1,0:T(8,128)(2,1)S(1)} %collective-permute-done.2.p1), channel_id=1, source_target_pairs={{0,8},{32,57},{8,0},{40,48},{16,24},{48,40},{24,16},{56,33},{1,9},... | collective-permute-start | bytes 294920 | tf_op jit(solution)/shard_map/ppermute | solution.py:39
  60.0 79.4 %collective-permute-start = (bf16[256,4096]{1,0:T(8,128)(2,1)}, bf16[256,4096]{1,0:T(8,128)(2,1)S(1)}, u32[]{:S(2)}, u32[]{:S(2)}) collective-permute-start(bf16[256,4096]{1,0:T(8,128)(2,1)} %other_half.1), channel_id=1, source_target_pairs={{0,32},{32,0},{1,33},{33,1},{2,34},{34,2},{3,35},{35,3},{4,36},{36... | collective-permute-start | bytes 6291464 | tf_op jit(solution)/shard_map/ppermute | solution.py:319
  65.3 53.9 %collective-permute-start.24 = (bf16[2,4,4,32,512]{4,3,2,1,0:T(8,128)(2,1)}, bf16[2,4,4,32,512]{4,3,2,1,0:T(8,128)(2,1)}, u32[]{:S(2)}, u32[]{:S(2)}) collective-permute-start(bf16[2,4,4,32,512]{4,3,2,1,0:T(8,128)(2,1)} %collective-permute-done.23.o1), channel_id=1, source_target_pairs={{0,8},{32,57},{8,0},{40,48},{16,24},{48,40},{24,16},{56,33},{1,9},... | collective-permute-start | bytes 3145736 | tf_op jit(solution)/shard_map/ppermute | solution.py:39
  75.7 6.7 %collective-permute-start.10 = (bf16[4,2,32,384]{3,2,1,0:T(8,128)(2,1)}, bf16[4,2,32,384]{3,2,1,0:T(8,128)(2,1)S(1)}, u32[]{:S(2)}, u32[]{:S(2)}) collective-permute-start(bf16[4,2,32,384]{3,2,1,0:T(8,128)(2,1)} %get-tuple-element.11.p0), channel_id=1, source_target_pairs={{0,64},{32,224},{64,0},{96,160},{128,192},{160,96},{192,128},{224,... | collective-permute-start | bytes 589832 | tf_op jit(solution)/shard_map/ppermute | solution.py:39
  78.5 6.4 %collective-permute-start.11 = (bf16[4,2,32,384]{3,2,1,0:T(8,128)(2,1)}, bf16[4,2,32,384]{3,2,1,0:T(8,128)(2,1)S(1)}, u32[]{:S(2)}, u32[]{:S(2)}) collective-permute-start(bf16[4,2,32,384]{3,2,1,0:T(8,128)(2,1)} %get-tuple-element.11.p0), channel_id=1, source_target_pairs={{0,192},{32,96},{64,128},{96,32},{128,64},{160,224},{192,0},{224,1... | collective-permute-start | bytes 589832 | tf_op jit(solution)/shard_map/ppermute | solution.py:39
  82.4 9.3 %collective-permute-start.5 = (bf16[4,2,32,384]{3,2,1,0:T(8,128)(2,1)}, bf16[4,2,32,384]{3,2,1,0:T(8,128)(2,1)S(1)}, u32[]{:S(2)}, u32[]{:S(2)}) collective-permute-start(bf16[4,2,32,384]{3,2,1,0:T(8,128)(2,1)} %get-tuple-element.10.p0), channel_id=1, source_target_pairs={{0,2},{32,38},{2,0},{34,36},{4,6},{36,34},{6,4},{38,32},{1,3},{33,... | collective-permute-start | bytes 589832 | tf_op jit(solution)/shard_map/ppermute | solution.py:39
  85.6 6.1 %collective-permute-start.6 = (bf16[4,2,32,384]{3,2,1,0:T(8,128)(2,1)}, bf16[4,2,32,384]{3,2,1,0:T(8,128)(2,1)S(1)}, u32[]{:S(2)}, u32[]{:S(2)}) collective-permute-start(bf16[4,2,32,384]{3,2,1,0:T(8,128)(2,1)} %get-tuple-element.10.p0), channel_id=1, source_target_pairs={{0,6},{32,34},{2,4},{34,32},{4,2},{36,38},{6,0},{38,36},{1,7},{33,... | collective-permute-start | bytes 589832 | tf_op jit(solution)/shard_map/ppermute | solution.py:39
  89.2 30.0 %collective-permute-start.13 = (bf16[4,4,2,32,384]{4,3,2,1,0:T(8,128)(2,1)}, bf16[4,4,2,32,384]{4,3,2,1,0:T(8,128)(2,1)}, u32[]{:S(2)}, u32[]{:S(2)}) collective-permute-start(bf16[4,4,2,32,384]{4,3,2,1,0:T(8,128)(2,1)} %shard_map.84.w0), channel_id=1, source_target_pairs={{0,2},{32,38},{2,0},{34,36},{4,6},{36,34},{6,4},{38,32},{1,3},{33,... | collective-permute-start | bytes 2359304 | tf_op jit(solution)/shard_map/ppermute | solution.py:39
  91.7 27.6 %collective-permute-start.16 = (bf16[4,4,2,32,384]{4,3,2,1,0:T(8,128)(2,1)}, bf16[4,4,2,32,384]{4,3,2,1,0:T(8,128)(2,1)}, u32[]{:S(2)}, u32[]{:S(2)}) collective-permute-start(bf16[4,4,2,32,384]{4,3,2,1,0:T(8,128)(2,1)} %shard_map.84.w0), channel_id=1, source_target_pairs={{0,6},{32,34},{2,4},{34,32},{4,2},{36,38},{6,0},{38,36},{1,7},{33,... | collective-permute-start | bytes 2359304 | tf_op jit(solution)/shard_map/ppermute | solution.py:39
  91.7 21.7 %collective-permute-start.7 = (bf16[4,2,32,384]{3,2,1,0:T(8,128)(2,1)S(1)}, bf16[4,2,32,384]{3,2,1,0:T(8,128)(2,1)}, u32[]{:S(2)}, u32[]{:S(2)}) collective-permute-start(bf16[4,2,32,384]{3,2,1,0:T(8,128)(2,1)S(1)} %collective-permute-done.5.p1), channel_id=1, source_target_pairs={{0,6},{32,34},{2,4},{34,32},{4,2},{36,38},{6,0},{38,36},{1,7},{33,... | collective-permute-start | bytes 589832 | tf_op jit(solution)/shard_map/ppermute | solution.py:39
  115.6 20.1 %collective-permute-start.8 = (bf16[4,4,2,32,384]{4,3,2,1,0:T(8,128)(2,1)}, bf16[4,4,2,32,384]{4,3,2,1,0:T(8,128)(2,1)}, u32[]{:S(2)}, u32[]{:S(2)}) collective-permute-start(bf16[4,4,2,32,384]{4,3,2,1,0:T(8,128)(2,1)} %shard_map.83.w0), channel_id=1, source_target_pairs={{0,64},{32,224},{64,0},{96,160},{128,192},{160,96},{192,128},{224,... | collective-permute-start | bytes 2359304 | tf_op jit(solution)/shard_map/ppermute | solution.py:39
  119.2 21.1 %collective-permute-start.25 = (bf16[2,4,4,32,512]{4,3,2,1,0:T(8,128)(2,1)}, bf16[2,4,4,32,512]{4,3,2,1,0:T(8,128)(2,1)}, u32[]{:S(2)}, u32[]{:S(2)}) collective-permute-start(bf16[2,4,4,32,512]{4,3,2,1,0:T(8,128)(2,1)} %collective-permute-done.24.o2), channel_id=1, source_target_pairs={{0,25},{32,40},{8,16},{40,32},{16,8},{48,56},{24,1},{56,48},{1,24}... | collective-permute-start | bytes 3145736 | tf_op jit(solution)/shard_map/ppermute | solution.py:39
  119.2 16.6 %collective-permute-start.15 = (bf16[4,4,2,32,384]{4,3,2,1,0:T(8,128)(2,1)}, bf16[4,4,2,32,384]{4,3,2,1,0:T(8,128)(2,1)S(1)}, u32[]{:S(2)}, u32[]{:S(2)}) collective-permute-start(bf16[4,4,2,32,384]{4,3,2,1,0:T(8,128)(2,1)} %shard_map.83.w0), channel_id=1, source_target_pairs={{0,192},{32,96},{64,128},{96,32},{128,64},{160,224},{192,0},{224,1... | collective-permute-start | bytes 2359304 | tf_op jit(solution)/shard_map/ppermute | solution.py:39
  119.3 20.9 %collective-permute-start.14 = (bf16[4,4,2,32,384]{4,3,2,1,0:T(8,128)(2,1)}, bf16[4,4,2,32,384]{4,3,2,1,0:T(8,128)(2,1)}, u32[]{:S(2)}, u32[]{:S(2)}) collective-permute-start(bf16[4,4,2,32,384]{4,3,2,1,0:T(8,128)(2,1)} %collective-permute-done.13.w1), channel_id=1, source_target_pairs={{0,6},{32,34},{2,4},{34,32},{4,2},{36,38},{6,0},{38,36},{1,7},{33,... | collective-permute-start | bytes 2359304 | tf_op jit(solution)/shard_map/ppermute | solution.py:39
  135.7 25.0 %collective-permute-start.9 = (bf16[4,4,2,32,384]{4,3,2,1,0:T(8,128)(2,1)}, bf16[4,4,2,32,384]{4,3,2,1,0:T(8,128)(2,1)}, u32[]{:S(2)}, u32[]{:S(2)}) collective-permute-start(bf16[4,4,2,32,384]{4,3,2,1,0:T(8,128)(2,1)} %collective-permute-done.8.w1), channel_id=1, source_target_pairs={{0,192},{32,96},{64,128},{96,32},{128,64},{160,224},{192,0},{224,1... | collective-permute-start | bytes 2359304 | tf_op jit(solution)/shard_map/ppermute | solution.py:39
  135.9 33.9 %collective-permute-start.26 = (bf16[2,4,4,32,512]{4,3,2,1,0:T(8,128)(2,1)S(1)}, bf16[2,4,4,32,512]{4,3,2,1,0:T(8,128)(2,1)}, u32[]{:S(2)}, u32[]{:S(2)}) collective-permute-start(bf16[2,4,4,32,512]{4,3,2,1,0:T(8,128)(2,1)S(1)} %maximum_select_fusion.o0), channel_id=1, source_target_pairs={{0,32},{32,0},{1,33},{33,1},{2,34},{34,2},{3,35},{35,3},{4,36},{36... | collective-permute-start | bytes 3145736 | tf_op jit(solution)/shard_map/ppermute | solution.py:319
  139.4 30.3 %collective-permute-start.27 = (bf16[2,4,4,32,512]{4,3,2,1,0:T(8,128)(2,1)}, bf16[2,4,4,32,512]{4,3,2,1,0:T(8,128)(2,1)}, u32[]{:S(2)}, u32[]{:S(2)}) collective-permute-start(bf16[2,4,4,32,512]{4,3,2,1,0:T(8,128)(2,1)} %collective-permute-done.23.o1), channel_id=1, source_target_pairs={{0,32},{32,0},{1,33},{33,1},{2,34},{34,2},{3,35},{35,3},{4,36},{36... | collective-permute-start | bytes 3145736 | tf_op jit(solution)/shard_map/ppermute | solution.py:319
  140.2 29.6 %collective-permute-start.28 = (bf16[2,4,4,32,512]{4,3,2,1,0:T(8,128)(2,1)}, bf16[2,4,4,32,512]{4,3,2,1,0:T(8,128)(2,1)}, u32[]{:S(2)}, u32[]{:S(2)}) collective-permute-start(bf16[2,4,4,32,512]{4,3,2,1,0:T(8,128)(2,1)} %collective-permute-done.24.o2), channel_id=1, source_target_pairs={{0,32},{32,0},{1,33},{33,1},{2,34},{34,2},{3,35},{35,3},{4,36},{36... | collective-permute-start | bytes 3145736 | tf_op jit(solution)/shard_map/ppermute | solution.py:319
  140.3 29.5 %collective-permute-start.29 = (bf16[2,4,4,32,512]{4,3,2,1,0:T(8,128)(2,1)}, bf16[2,4,4,32,512]{4,3,2,1,0:T(8,128)(2,1)}, u32[]{:S(2)}, u32[]{:S(2)}) collective-permute-start(bf16[2,4,4,32,512]{4,3,2,1,0:T(8,128)(2,1)} %collective-permute-done.25.o3), channel_id=1, source_target_pairs={{0,32},{32,0},{1,33},{33,1},{2,34},{34,2},{3,35},{35,3},{4,36},{36... | collective-permute-start | bytes 3145736 | tf_op jit(solution)/shard_map/ppermute | solution.py:319
  (22 other events, 256.9 us)
where the time goes:
time: 181 us; the launch traced here: 180 us
  waiting for transfers between devices  79.6 us (44%)
  Pallas kernels  43.5 us (24%)
  starting transfers between devices  43.2 us (24%)
  other arithmetic  9.23 us (5%)
  local copies, waits for them, and re-layouts  4.4 us (2%)
    ppermute x24, waiting for transfers between devices, exchange(): return lax.ppermute(block, names, pairs)  79.6 us
    ppermute x24, starting transfers between devices, exchange(): return lax.ppermute(block, names, pairs)  32.6 us
    pallas_call x2, Pallas kernels, first_products(): pl.pallas_call(functools.partial(first_kernel, colour), in_specs=[pl.Bloc...  10.9 us
    ppermute x6, starting transfers between devices, swap(): return lax.ppermute(a, 'c', [(0, 1), (1, 0)])  10.7 us
    pallas_call x1, Pallas kernels, body(): pl.pallas_call(finish_kernel, in_specs=[smem] + [vmem] * 6 + [hbm] * 9, o...  9.59 us
    pallas_call x4, Pallas kernels, local(): pl.pallas_call(kernel, in_specs=[pl.BlockSpec(memory_space=pltpu.SMEM)] +...  8.08 us
    pallas_call x1, Pallas kernels, body(): pl.pallas_call(prepare_kernel, in_specs=[smem, hbm, hbm], out_specs=vmem,...  5.88 us
    pallas_call x1, Pallas kernels, last_products(): pl.pallas_call(last_kernel, in_specs=[pl.BlockSpec(memory_space=pltpu.SME...  5.43 us
  transfers between devices with their start and end apart: 30, of which 13 were waited for; matrix products, arithmetic and copies ran while one was open for 4% of the time, Pallas kernels for 18%

commit v1 on v0

--- a/solution.py
+++ b/solution.py
@@ -12,6 +12,7 @@
 AXES = ("y", "c", "zl", "x", "zh")
 NY, NC, NZL, NX, NZH = 4, 2, 4, 4, 2
 RING = {"x": (("c", "x"), 4), "y": (("y", "c"), 4), "z": (("c", "zl", "zh"), 8)}
+VMEM_LIMIT = pltpu.CompilerParams(vmem_limit_bytes=20 * 1024 * 1024)
 HD = 128
 ROWS = 32
 T = 256
@@ -111,6 +112,7 @@
         in_specs=[pl.BlockSpec(memory_space=pltpu.SMEM)] + [vmem] * len(arrays),
         out_specs=[vmem] * len(out),
         out_shape=out,
+        compiler_params=VMEM_LIMIT,
     )(tab, *arrays)
 
 
@@ -142,6 +144,21 @@
             xp_ref.at[:, pl.ds(pl.multiple_of(y * 1024, 1024), 1024)], dst.at[pl.ds(T, T)], sems[1]
         ),
     ]
+
+
+def rms_kernel(x_ref, kept_ref, inv_ref, sem):
+    loads = [
+        pltpu.make_async_copy(x_ref.at[:, pl.ds(k * 1024, 1024)], kept_ref.at[k], sem.at[k]) for k in range(8)
+    ]
+    for c in loads:
+        c.start()
+    total = jnp.zeros((T, 128), jnp.float32)
+    for k, c in enumerate(loads):
+        c.wait()
+        for n in range(8):
+            v = kept_ref[k, :, n * 128 : n * 128 + 128].astype(jnp.float32)
+            total += v * v
+    inv_ref[...] = lax.rsqrt(jnp.sum(total, -1, keepdims=True) * (1.0 / 8192) + 1e-05)
 
 
 def prepare_kernel(tab, x_ref, xp_ref, xb_ref, ps, sem):
@@ -225,6 +242,7 @@
             pltpu.VMEM((3, *WEIGHTS[colour]), jnp.bfloat16),
             pltpu.SemaphoreType.DMA((9,)),
         ],
+        compiler_params=VMEM_LIMIT,
     )(tab, *xs, *w)
 
 
@@ -243,15 +261,15 @@
             pltpu.SemaphoreType.DMA((6,)),
             pltpu.SemaphoreType.DMA((2,)),
         ],
+        compiler_params=VMEM_LIMIT,
         name="last",
     )(tab, *xs, a, b, ta, tb)
 
 
 def finish_kernel(
     tab, own_ref, par_ref, inv_ref, cos_ref, sin_ref, mask_ref, x_ref,
-    o0, o1, o2, o3, p0, p1, p2, p3, out_ref, ot, xs, ys, mixed, sem, ysem,
+    o0, o1, o2, o3, p0, p1, p2, p3, out_ref, ot, ys, mixed, sem, ysem,
 ):
-    pltpu.make_async_copy(x_ref, xs, sem.at[0]).start()
     core = tab[CORE]
     for at, pieces, c in ((Z, (o0, o1, o2, o3), core), (ZP, (p0, p1, p2, p3), 1 - core)):
         for n, piece in enumerate(pieces):
@@ -278,7 +296,6 @@
         mixed[:, h * HD : h * HD + HD] = jnp.dot(
             probs, values, preferred_element_type=jnp.float32
         ).astype(jnp.bfloat16)
-    pltpu.make_async_copy(xs, xs, sem.at[0]).wait()
     pltpu.make_async_copy(ot, ot, sem.at[1]).wait()
     writes = []
     for k in range(NY * NC):
@@ -286,7 +303,7 @@
         branch = lax.dot_general(
             mixed[...], rows, (((1,), (1,)), ((), ())), preferred_element_type=jnp.float32
         )
-        ys[k] = (xs[:, k * 1024 : k * 1024 + 1024].astype(jnp.float32) + branch).astype(jnp.bfloat16)
+        ys[k] = (x_ref[k].astype(jnp.float32) + branch).astype(jnp.bfloat16)
         writes.append(pltpu.make_async_copy(ys.at[k], out_ref.at[:, pl.ds(k * 1024, 1024)], ysem.at[k]))
         writes[-1].start()
     for w in writes:
@@ -334,6 +351,7 @@
         out_specs=vmem,
         out_shape=jax.ShapeDtypeStruct((T, 4096), jnp.bfloat16),
         scratch_shapes=[pltpu.SemaphoreType.DMA((NY,))],
+        compiler_params=VMEM_LIMIT,
         name="other_half",
     )(tab, stream)
     x_par = swap(x_par)
@@ -346,10 +364,18 @@
             pltpu.VMEM((4, 2 * T, 1024), jnp.bfloat16),
             pltpu.SemaphoreType.DMA((8,)),
         ],
+        compiler_params=VMEM_LIMIT,
         name="prepare",
     )(tab, stream, x_par)
-    wide = stream.astype(jnp.float32)
-    inv = lax.rsqrt(jnp.mean(wide * wide, -1, keepdims=True) + 1e-05)
+    kept, inv = pl.pallas_call(
+        rms_kernel,
+        in_specs=[hbm],
+        out_specs=[vmem, vmem],
+        out_shape=[pltpu.VMEM((8, T, 1024), jnp.bfloat16), jax.ShapeDtypeStruct((T, 1), jnp.float32)],
+        scratch_shapes=[pltpu.SemaphoreType.DMA((8,))],
+        compiler_params=VMEM_LIMIT,
+        name="rms",
+    )(stream)
     xs = (stream, x_par, x_cut)
     total_a = first_products("a", tab, xs, a[:3])
     total_b = first_products("b", tab, xs, b[:3])
@@ -357,19 +383,19 @@
     par = swap(par)
     return pl.pallas_call(
         finish_kernel,
-        in_specs=[smem] + [vmem] * 6 + [hbm] * 9,
+        in_specs=[smem] + [vmem] * 7 + [hbm] * 8,
         out_specs=hbm,
         out_shape=jax.ShapeDtypeStruct((T, 8192), jnp.bfloat16),
         scratch_shapes=[
             pltpu.VMEM((NY, NC, NZL, NX, NZH, ROWS, 512), jnp.bfloat16),
-            pltpu.VMEM((T, 8192), jnp.bfloat16),
             pltpu.VMEM((NY * NC, T, 1024), jnp.bfloat16),
             pltpu.VMEM((T, 512), jnp.bfloat16),
             pltpu.SemaphoreType.DMA((2,)),
             pltpu.SemaphoreType.DMA((NY * NC,)),
         ],
+        compiler_params=VMEM_LIMIT,
         name="finish",
-    )(tab, own, par, inv, cos, sin, mask, stream, *o, *o_par)
+    )(tab, own, par, inv, cos, sin, mask, kept, *o, *o_par)
 
 
 def solution(mesh):

time: 181 us -> 156 us (0.86)
  Pallas kernels: 43.5 us -> 25.6 us
  other arithmetic: 9.23 us -> 3.45 us
  waiting for transfers between devices: 79.6 us -> 81.8 us
  local copies, waits for them, and re-layouts: 4.4 us -> 2.29 us
    pallas_call x4, Pallas kernels: 8.08 us -> 2.41 us  [local(): pl.pallas_call(kernel, in_specs=[pl.BlockSpec(memory_space=pltpu.SMEM)] +...]
    pallas_call x2, Pallas kernels: 10.9 us -> 6.61 us  [first_products(): pl.pallas_call(functools.partial(first_kernel, colour), in_specs=[pl.Bloc...]
    reduce_sum x1 -> x0, other arithmetic: 3.1 us -> none  [body(): inv = lax.rsqrt(jnp.mean(wide * wide, -1, keepdims=True) + 1e-05)]
    pallas_call x1, Pallas kernels: 5.88 us -> 2.94 us  [body(): pl.pallas_call(prepare_kernel, in_specs=[smem, hbm, hbm], out_specs=vmem,...]
    pallas_call x1, Pallas kernels: 3.54 us -> 0.77 us  [body(): pl.pallas_call(other_half_kernel, in_specs=[smem, hbm], out_specs=vmem, o...]
    pallas_call x1, Pallas kernels: 5.43 us -> 2.94 us  [last_products(): pl.pallas_call(last_kernel, in_specs=[pl.BlockSpec(memory_space=pltpu.SME...]
    ppermute x24, waiting for transfers between devices: 79.6 us -> 81.8 us  [exchange(): return lax.ppermute(block, names, pairs)]
    pallas_call x1 -> x2, Pallas kernels: 9.59 us -> 9.9 us  [the longest x1 8.26 us: body(): pl.pallas_call(finish_kernel, in_specs=[smem] + [vmem] * 7 + [hbm] * 8, o...]
  transfers between devices with their start and end apart: 30 -> 30, of which waited for: 13 -> 13; matrix products, arithmetic and copies ran while one was open for 4% -> 1% of each run, Pallas kernels for 18% -> 11%
where the time goes in v1:
time: 156 us
  waiting for transfers between devices  81.8 us (52%)
  starting transfers between devices  42.1 us (27%)
  Pallas kernels  25.6 us (16%)
  other arithmetic  3.45 us (2%)
  local copies, waits for them, and re-layouts  2.29 us (1%)
    ppermute x24, waiting for transfers between devices, exchange(): return lax.ppermute(block, names, pairs)  81.8 us
    ppermute x24, starting transfers between devices, exchange(): return lax.ppermute(block, names, pairs)  33.2 us
    ppermute x6, starting transfers between devices, swap(): return lax.ppermute(a, 'c', [(0, 1), (1, 0)])  8.93 us
    pallas_call x1, Pallas kernels, body(): pl.pallas_call(finish_kernel, in_specs=[smem] + [vmem] * 7 + [hbm] * 8, o...  8.26 us
    pallas_call x2, Pallas kernels, first_products(): pl.pallas_call(functools.partial(first_kernel, colour), in_specs=[pl.Bloc...  6.61 us
  transfers between devices with their start and end apart: 30, of which 13 were waited for; matrix products, arithmetic and copies ran while one was open for 1% of the time, Pallas kernels for 11%

profile of v1, /device:TPU:1, one launch (start us, length us, event | category | flops | bytes accessed | tf_op | source)
XLA Modules:
  0.0 155.7 jit_solution(16373912838640227690)
XLA Ops:
  1.5 3.3 %collective-permute-start.18 = (bf16[32,512]{1,0:T(8,128)(2,1)}, bf16[32,512]{1,0:T(8,128)(2,1)S(1)}, u32[]{:S(2)}, u32[]{:S(2)}) collective-permute-start(bf16[32,512]{1,0:T(8,128)(2,1)} %bitcast.25), channel_id=1, source_target_pairs={{0,2},{32,38},{2,0},{34,36},{4,6},{36,34},{6,4},{38,32},{1,3},{33,... | collective-permute-start | bytes 98312 | tf_op jit(solution)/shard_map/ppermute | solution.py:40
  7.5 2.9 %collective-permute-done.19 = bf16[2,32,512]{2,1,0:T(8,128)(2,1)S(1)} collective-permute-done((bf16[2,32,512]{2,1,0:T(8,128)(2,1)S(1)}, bf16[2,32,512]{2,1,0:T(8,128)(2,1)S(1)}, u32[]{:S(2)}, u32[]{:S(2)}) %collective-permute-start.19) | collective-permute-done | bytes 65568 | tf_op jit(solution)/shard_map/ppermute | solution.py:40
  10.5 3.0 %collective-permute-start.20 = (bf16[4,32,512]{2,1,0:T(8,128)(2,1)S(1)}, bf16[4,32,512]{2,1,0:T(8,128)(2,1)S(1)}, u32[]{:S(2)}, u32[]{:S(2)}) collective-permute-start(bf16[4,32,512]{2,1,0:T(8,128)(2,1)S(1)} %get-tuple-element.20), channel_id=1, source_target_pairs={{0,64},{32,224},{64,0},{96,160},{128,192},{160,96},{192,128},{224,... | collective-permute-start | bytes 393224 | tf_op jit(solution)/shard_map/ppermute | solution.py:40
  16.1 6.4 %collective-permute-done.21.p1 = bf16[2,4,32,512]{3,2,1,0:T(8,128)(2,1)S(1)} collective-permute-done((bf16[2,4,32,512]{3,2,1,0:T(8,128)(2,1)S(1)}, bf16[2,4,32,512]{3,2,1,0:T(8,128)(2,1)S(1)}, u32[]{:S(2)}, u32[]{:S(2)}) %collective-permute-start.21) | collective-permute-done | bytes 262176 | tf_op jit(solution)/shard_map/ppermute | solution.py:40
  23.1 4.3 %collective-permute-start.22 = (bf16[4,4,32,512]{3,2,1,0:T(8,128)(2,1)S(1)}, bf16[4,4,32,512]{3,2,1,0:T(8,128)(2,1)S(1)}, u32[]{:S(2)}, u32[]{:S(2)}) collective-permute-start(bf16[4,4,32,512]{3,2,1,0:T(8,128)(2,1)S(1)} %shard_map.87), channel_id=1, source_target_pairs={{0,8},{32,57},{8,0},{40,48},{16,24},{48,40},{24,16},{56,33},{1,9},... | collective-permute-start | bytes 1572872 | tf_op jit(solution)/shard_map/ppermute | solution.py:40
  27.4 6.6 %collective-permute-done.22 = bf16[4,4,32,512]{3,2,1,0:T(8,128)(2,1)S(1)} collective-permute-done((bf16[4,4,32,512]{3,2,1,0:T(8,128)(2,1)S(1)}, bf16[4,4,32,512]{3,2,1,0:T(8,128)(2,1)S(1)}, u32[]{:S(2)}, u32[]{:S(2)}) %collective-permute-start.22) | collective-permute-done | bytes 524320 | tf_op jit(solution)/shard_map/ppermute | solution.py:40
  34.3 2.8 %collective-permute-start.1 = (bf16[32,768]{1,0:T(8,128)(2,1)S(1)}, bf16[32,768]{1,0:T(8,128)(2,1)S(1)}, u32[]{:S(2)}, u32[]{:S(2)}) collective-permute-start(bf16[32,768]{1,0:T(8,128)(2,1)S(1)} %multiply_convert_fusion), channel_id=1, source_target_pairs={{0,8},{32,57},{8,0},{40,48},{16,24},{48,40},{24,16},{56,33},{1,9},... | collective-permute-start | bytes 147464 | tf_op jit(solution)/shard_map/ppermute | solution.py:40
  39.1 12.6 %collective-permute-done.2.p1 = bf16[2,32,768]{2,1,0:T(8,128)(2,1)S(1)} collective-permute-done((bf16[2,32,768]{2,1,0:T(8,128)(2,1)S(1)}, bf16[2,32,768]{2,1,0:T(8,128)(2,1)S(1)}, u32[]{:S(2)}, u32[]{:S(2)}) %collective-permute-start.2) | collective-permute-done | bytes 98336 | tf_op jit(solution)/shard_map/ppermute | solution.py:40
  51.7 2.5 %collective-permute-start.3 = (bf16[2,32,768]{2,1,0:T(8,128)(2,1)S(1)}, bf16[2,32,768]{2,1,0:T(8,128)(2,1)S(1)}, u32[]{:S(2)}, u32[]{:S(2)}) collective-permute-start(bf16[2,32,768]{2,1,0:T(8,128)(2,1)S(1)} %collective-permute-done.2.p1), channel_id=1, source_target_pairs={{0,8},{32,57},{8,0},{40,48},{16,24},{48,40},{24,16},{56,33},{1,9},... | collective-permute-start | bytes 294920 | tf_op jit(solution)/shard_map/ppermute | solution.py:40
  57.2 5.4 %collective-permute-start = (bf16[256,4096]{1,0:T(8,128)(2,1)S(1)}, bf16[256,4096]{1,0:T(8,128)(2,1)S(1)}, u32[]{:S(2)}, u32[]{:S(2)}) collective-permute-start(bf16[256,4096]{1,0:T(8,128)(2,1)S(1)} %other_half.1), channel_id=1, source_target_pairs={{0,32},{32,0},{1,33},{33,1},{2,34},{34,2},{3,35},{35,3},{4,36},{36... | collective-permute-start | bytes 6291464 | tf_op jit(solution)/shard_map/ppermute | solution.py:336
  62.6 2.9 %collective-permute-start.24 = (bf16[2,4,4,32,512]{4,3,2,1,0:T(8,128)(2,1)S(1)}, bf16[2,4,4,32,512]{4,3,2,1,0:T(8,128)(2,1)S(1)}, u32[]{:S(2)}, u32[]{:S(2)}) collective-permute-start(bf16[2,4,4,32,512]{4,3,2,1,0:T(8,128)(2,1)S(1)} %collective-permute-done.23.o1), channel_id=1, source_target_pairs={{0,8},{32,57},{8,0},{40,48},{16,24},{48,40},{24,16},{56,33},{1,9},... | collective-permute-start | bytes 3145736 | tf_op jit(solution)/shard_map/ppermute | solution.py:40
  65.6 4.8 %collective-permute-done.4.p3 = bf16[2,32,768]{2,1,0:T(8,128)(2,1)S(1)} collective-permute-done((bf16[2,32,768]{2,1,0:T(8,128)(2,1)S(1)}, bf16[2,32,768]{2,1,0:T(8,128)(2,1)S(1)}, u32[]{:S(2)}, u32[]{:S(2)}) %collective-permute-start.4) | collective-permute-done | bytes 98336 | tf_op jit(solution)/shard_map/ppermute | solution.py:40
  71.0 2.9 %collective-permute-start.10 = (bf16[4,2,32,384]{3,2,1,0:T(8,128)(2,1)S(1)}, bf16[4,2,32,384]{3,2,1,0:T(8,128)(2,1)S(1)}, u32[]{:S(2)}, u32[]{:S(2)}) collective-permute-start(bf16[4,2,32,384]{3,2,1,0:T(8,128)(2,1)S(1)} %get-tuple-element.13.p0), channel_id=1, source_target_pairs={{0,64},{32,224},{64,0},{96,160},{128,192},{160,96},{192,128},{224,... | collective-permute-start | bytes 589832 | tf_op jit(solution)/shard_map/ppermute | solution.py:40
  73.9 3.4 %collective-permute-done.10.p1 = bf16[4,2,32,384]{3,2,1,0:T(8,128)(2,1)S(1)} collective-permute-done((bf16[4,2,32,384]{3,2,1,0:T(8,128)(2,1)S(1)}, bf16[4,2,32,384]{3,2,1,0:T(8,128)(2,1)S(1)}, u32[]{:S(2)}, u32[]{:S(2)}) %collective-permute-start.10) | collective-permute-done | bytes 196640 | tf_op jit(solution)/shard_map/ppermute | solution.py:40
  77.3 2.5 %collective-permute-start.5 = (bf16[4,2,32,384]{3,2,1,0:T(8,128)(2,1)S(1)}, bf16[4,2,32,384]{3,2,1,0:T(8,128)(2,1)S(1)}, u32[]{:S(2)}, u32[]{:S(2)}) collective-permute-start(bf16[4,2,32,384]{3,2,1,0:T(8,128)(2,1)S(1)} %get-tuple-element.12.p0), channel_id=1, source_target_pairs={{0,2},{32,38},{2,0},{34,36},{4,6},{36,34},{6,4},{38,32},{1,3},{33,... | collective-permute-start | bytes 589832 | tf_op jit(solution)/shard_map/ppermute | solution.py:40
  82.4 2.6 %collective-permute-start.13 = (bf16[4,4,2,32,384]{4,3,2,1,0:T(8,128)(2,1)S(1)}, bf16[4,4,2,32,384]{4,3,2,1,0:T(8,128)(2,1)S(1)}, u32[]{:S(2)}, u32[]{:S(2)}) collective-permute-start(bf16[4,4,2,32,384]{4,3,2,1,0:T(8,128)(2,1)S(1)} %shard_map.84.w0), channel_id=1, source_target_pairs={{0,2},{32,38},{2,0},{34,36},{4,6},{36,34},{6,4},{38,32},{1,3},{33,... | collective-permute-start | bytes 2359304 | tf_op jit(solution)/shard_map/ppermute | solution.py:40
  86.5 20.2 %collective-permute-done.7.p3 = bf16[4,2,32,384]{3,2,1,0:T(8,128)(2,1)S(1)} collective-permute-done((bf16[4,2,32,384]{3,2,1,0:T(8,128)(2,1)S(1)}, bf16[4,2,32,384]{3,2,1,0:T(8,128)(2,1)S(1)}, u32[]{:S(2)}, u32[]{:S(2)}) %collective-permute-start.7) | collective-permute-done | bytes 196640 | tf_op jit(solution)/shard_map/ppermute | solution.py:40
  107.3 3.7 %collective-permute-start.8 = (bf16[4,4,2,32,384]{4,3,2,1,0:T(8,128)(2,1)S(1)}, bf16[4,4,2,32,384]{4,3,2,1,0:T(8,128)(2,1)S(1)}, u32[]{:S(2)}, u32[]{:S(2)}) collective-permute-start(bf16[4,4,2,32,384]{4,3,2,1,0:T(8,128)(2,1)S(1)} %shard_map.83.w0), channel_id=1, source_target_pairs={{0,64},{32,224},{64,0},{96,160},{128,192},{160,96},{192,128},{224,... | collective-permute-start | bytes 2359304 | tf_op jit(solution)/shard_map/ppermute | solution.py:40
  111.2 15.5 %collective-permute-done.8.w1 = bf16[4,4,2,32,384]{4,3,2,1,0:T(8,128)(2,1)S(1)} collective-permute-done((bf16[4,4,2,32,384]{4,3,2,1,0:T(8,128)(2,1)S(1)}, bf16[4,4,2,32,384]{4,3,2,1,0:T(8,128)(2,1)S(1)}, u32[]{:S(2)}, u32[]{:S(2)}) %collective-permute-start.8) | collective-permute-done | bytes 786464 | tf_op jit(solution)/shard_map/ppermute | solution.py:40
  131.4 2.9 %prepare.1.xb_ref = bf16[4,512,1024]{2,1,0:T(8,128)(2,1)S(1)} custom-call(s32[33]{0:T(128)S(1)} %concatenate.15.tab, bf16[256,8192]{1,0:T(8,128)(2,1)S(1)} %copy-done.1, bf16[256,4096]{1,0:T(8,128)(2,1)S(1)} %collective-permute-done.xp_ref), custom_call_target="tpu_custom_call" | custom-call | tf_op jit(solution)/shard_map/prepare/pallas_call | solution.py:358
  134.3 3.0 %shard_map.86.tb_ref = f32[512,384]{1,0:T(8,128)S(1)} custom-call(s32[33]{0:T(128)S(1)} %concatenate.15.tab, bf16[256,8192]{1,0:T(8,128)(2,1)S(1)} %copy-done.1, bf16[256,4096]{1,0:T(8,128)(2,1)S(1)} %collective-permute-done.xp_ref, bf16[4,512,1024]{2,1,0:T(8,128)(2,1)S(1)} %prepare.1.xb_ref, bf16[4,4,2,32,384]{4,3,2,1,0:T(8,128)(2,1)S(1)} %shard_map.84.w0, ...), custom_call_target="tpu_custom_call" | custom-call | tf_op jit(solution)/shard_map/pallas_call | solution.py:235
  137.3 3.6 %shard_map.85.ta_ref = f32[512,384]{1,0:T(8,128)S(1)} custom-call(s32[33]{0:T(128)S(1)} %concatenate.15.tab, bf16[256,8192]{1,0:T(8,128)(2,1)S(1)} %copy-done.1, bf16[256,4096]{1,0:T(8,128)(2,1)S(1)} %collective-permute-done.xp_ref, bf16[4,512,1024]{2,1,0:T(8,128)(2,1)S(1)} %prepare.1.xb_ref, bf16[4,4,2,32,384]{4,3,2,1,0:T(8,128)(2,1)S(1)} %shard_map.83.w0, ...), custom_call_target="tpu_custom_call" | custom-call | tf_op jit(solution)/shard_map/pallas_call | solution.py:235
  141.0 2.9 %last.1 = (f32[256,768]{1,0:T(8,128)S(1)}, f32[256,768]{1,0:T(8,128)S(1)}) custom-call(s32[33]{0:T(128)S(1)} %concatenate.15.tab, bf16[256,8192]{1,0:T(8,128)(2,1)S(1)} %copy-done.1, bf16[256,4096]{1,0:T(8,128)(2,1)S(1)} %collective-permute-done.xp_ref, bf16[4,512,1024]{2,1,0:T(8,128)(2,1)S(1)} %prepare.1.xb_ref, ...), custom_call_target="tpu_custom_call" | custom-call | tf_op jit(solution)/shard_map/last/pallas_call | solution.py:251
  147.2 8.3 %finish.1 = bf16[256,8192]{1,0:T(8,128)(2,1)} custom-call(s32[33]{0:T(128)S(1)} %concatenate.15.tab, f32[256,768]{1,0:T(8,128)S(1)} %get-tuple-element.14.own_ref, f32[256,768]{1,0:T(8,128)S(1)} %collective-permute-done.17.par_ref, f32[256,1]{1,0:T(8,128)S(1)} %get-tuple-element.16.inv_ref, f32[256,128]{1,0:T(8,128)S(1)} %get-tuple-element.30.cos_ref, ...), custom_call_target="tpu_custom_call" | custom-call | tf_op jit(solution)/shard_map/finish/pallas_call | solution.py:384
  (71 shorter events, 26.0 us)
Async XLA Ops:
  10.5 5.4 %collective-permute-start.20 = (bf16[4,32,512]{2,1,0:T(8,128)(2,1)S(1)}, bf16[4,32,512]{2,1,0:T(8,128)(2,1)S(1)}, u32[]{:S(2)}, u32[]{:S(2)}) collective-permute-start(bf16[4,32,512]{2,1,0:T(8,128)(2,1)S(1)} %get-tuple-element.20), channel_id=1, source_target_pairs={{0,64},{32,224},{64,0},{96,160},{128,192},{160,96},{192,128},{224,... | collective-permute-start | bytes 393224 | tf_op jit(solution)/shard_map/ppermute | solution.py:40
  15.9 6.6 %collective-permute-start.21 = (bf16[2,4,32,512]{3,2,1,0:T(8,128)(2,1)S(1)}, bf16[2,4,32,512]{3,2,1,0:T(8,128)(2,1)S(1)}, u32[]{:S(2)}, u32[]{:S(2)}) collective-permute-start(bf16[2,4,32,512]{3,2,1,0:T(8,128)(2,1)S(1)} %maximum_select_fusion.1.p0), channel_id=1, source_target_pairs={{0,192},{32,96},{64,128},{96,32},{128,64},{160,224},{192,0},{224,1... | collective-permute-start | bytes 786440 | tf_op jit(solution)/shard_map/ppermute | solution.py:40
  23.1 10.9 %collective-permute-start.22 = (bf16[4,4,32,512]{3,2,1,0:T(8,128)(2,1)S(1)}, bf16[4,4,32,512]{3,2,1,0:T(8,128)(2,1)S(1)}, u32[]{:S(2)}, u32[]{:S(2)}) collective-permute-start(bf16[4,4,32,512]{3,2,1,0:T(8,128)(2,1)S(1)} %shard_map.87), channel_id=1, source_target_pairs={{0,8},{32,57},{8,0},{40,48},{16,24},{48,40},{24,16},{56,33},{1,9},... | collective-permute-start | bytes 1572872 | tf_op jit(solution)/shard_map/ppermute | solution.py:40
  34.2 28.5 %collective-permute-start.23 = (bf16[2,4,4,32,512]{4,3,2,1,0:T(8,128)(2,1)S(1)}, bf16[2,4,4,32,512]{4,3,2,1,0:T(8,128)(2,1)S(1)}, u32[]{:S(2)}, u32[]{:S(2)}) collective-permute-start(bf16[2,4,4,32,512]{4,3,2,1,0:T(8,128)(2,1)S(1)} %maximum_select_fusion.o0), channel_id=1, source_target_pairs={{0,25},{32,40},{8,16},{40,32},{16,8},{48,56},{24,1},{56,48},{1,24}... | collective-permute-start | bytes 3145736 | tf_op jit(solution)/shard_map/ppermute | solution.py:40
  38.5 13.2 %collective-permute-start.2 = (bf16[2,32,768]{2,1,0:T(8,128)(2,1)S(1)}, bf16[2,32,768]{2,1,0:T(8,128)(2,1)S(1)}, u32[]{:S(2)}, u32[]{:S(2)}) collective-permute-start(bf16[2,32,768]{2,1,0:T(8,128)(2,1)S(1)} %maximum_select_fusion.2.p0), channel_id=1, source_target_pairs={{0,25},{32,40},{8,16},{40,32},{16,8},{48,56},{24,1},{56,48},{1,24}... | collective-permute-start | bytes 294920 | tf_op jit(solution)/shard_map/ppermute | solution.py:40
  51.7 13.9 %collective-permute-start.3 = (bf16[2,32,768]{2,1,0:T(8,128)(2,1)S(1)}, bf16[2,32,768]{2,1,0:T(8,128)(2,1)S(1)}, u32[]{:S(2)}, u32[]{:S(2)}) collective-permute-start(bf16[2,32,768]{2,1,0:T(8,128)(2,1)S(1)} %collective-permute-done.2.p1), channel_id=1, source_target_pairs={{0,8},{32,57},{8,0},{40,48},{16,24},{48,40},{24,16},{56,33},{1,9},... | collective-permute-start | bytes 294920 | tf_op jit(solution)/shard_map/ppermute | solution.py:40
  57.2 73.6 %collective-permute-start = (bf16[256,4096]{1,0:T(8,128)(2,1)S(1)}, bf16[256,4096]{1,0:T(8,128)(2,1)S(1)}, u32[]{:S(2)}, u32[]{:S(2)}) collective-permute-start(bf16[256,4096]{1,0:T(8,128)(2,1)S(1)} %other_half.1), channel_id=1, source_target_pairs={{0,32},{32,0},{1,33},{33,1},{2,34},{34,2},{3,35},{35,3},{4,36},{36... | collective-permute-start | bytes 6291464 | tf_op jit(solution)/shard_map/ppermute | solution.py:336
  62.6 48.3 %collective-permute-start.24 = (bf16[2,4,4,32,512]{4,3,2,1,0:T(8,128)(2,1)S(1)}, bf16[2,4,4,32,512]{4,3,2,1,0:T(8,128)(2,1)S(1)}, u32[]{:S(2)}, u32[]{:S(2)}) collective-permute-start(bf16[2,4,4,32,512]{4,3,2,1,0:T(8,128)(2,1)S(1)} %collective-permute-done.23.o1), channel_id=1, source_target_pairs={{0,8},{32,57},{8,0},{40,48},{16,24},{48,40},{24,16},{56,33},{1,9},... | collective-permute-start | bytes 3145736 | tf_op jit(solution)/shard_map/ppermute | solution.py:40
  71.0 6.3 %collective-permute-start.10 = (bf16[4,2,32,384]{3,2,1,0:T(8,128)(2,1)S(1)}, bf16[4,2,32,384]{3,2,1,0:T(8,128)(2,1)S(1)}, u32[]{:S(2)}, u32[]{:S(2)}) collective-permute-start(bf16[4,2,32,384]{3,2,1,0:T(8,128)(2,1)S(1)} %get-tuple-element.13.p0), channel_id=1, source_target_pairs={{0,64},{32,224},{64,0},{96,160},{128,192},{160,96},{192,128},{224,... | collective-permute-start | bytes 589832 | tf_op jit(solution)/shard_map/ppermute | solution.py:40
  73.9 5.9 %collective-permute-start.11 = (bf16[4,2,32,384]{3,2,1,0:T(8,128)(2,1)S(1)}, bf16[4,2,32,384]{3,2,1,0:T(8,128)(2,1)S(1)}, u32[]{:S(2)}, u32[]{:S(2)}) collective-permute-start(bf16[4,2,32,384]{3,2,1,0:T(8,128)(2,1)S(1)} %get-tuple-element.13.p0), channel_id=1, source_target_pairs={{0,192},{32,96},{64,128},{96,32},{128,64},{160,224},{192,0},{224,1... | collective-permute-start | bytes 589832 | tf_op jit(solution)/shard_map/ppermute | solution.py:40
  77.3 7.7 %collective-permute-start.5 = (bf16[4,2,32,384]{3,2,1,0:T(8,128)(2,1)S(1)}, bf16[4,2,32,384]{3,2,1,0:T(8,128)(2,1)S(1)}, u32[]{:S(2)}, u32[]{:S(2)}) collective-permute-start(bf16[4,2,32,384]{3,2,1,0:T(8,128)(2,1)S(1)} %get-tuple-element.12.p0), channel_id=1, source_target_pairs={{0,2},{32,38},{2,0},{34,36},{4,6},{36,34},{6,4},{38,32},{1,3},{33,... | collective-permute-start | bytes 589832 | tf_op jit(solution)/shard_map/ppermute | solution.py:40
  79.8 5.2 %collective-permute-start.6 = (bf16[4,2,32,384]{3,2,1,0:T(8,128)(2,1)S(1)}, bf16[4,2,32,384]{3,2,1,0:T(8,128)(2,1)S(1)}, u32[]{:S(2)}, u32[]{:S(2)}) collective-permute-start(bf16[4,2,32,384]{3,2,1,0:T(8,128)(2,1)S(1)} %get-tuple-element.12.p0), channel_id=1, source_target_pairs={{0,6},{32,34},{2,4},{34,32},{4,2},{36,38},{6,0},{38,36},{1,7},{33,... | collective-permute-start | bytes 589832 | tf_op jit(solution)/shard_map/ppermute | solution.py:40
  82.4 28.6 %collective-permute-start.13 = (bf16[4,4,2,32,384]{4,3,2,1,0:T(8,128)(2,1)S(1)}, bf16[4,4,2,32,384]{4,3,2,1,0:T(8,128)(2,1)S(1)}, u32[]{:S(2)}, u32[]{:S(2)}) collective-permute-start(bf16[4,4,2,32,384]{4,3,2,1,0:T(8,128)(2,1)S(1)} %shard_map.84.w0), channel_id=1, source_target_pairs={{0,2},{32,38},{2,0},{34,36},{4,6},{36,34},{6,4},{38,32},{1,3},{33,... | collective-permute-start | bytes 2359304 | tf_op jit(solution)/shard_map/ppermute | solution.py:40
  85.0 26.1 %collective-permute-start.16 = (bf16[4,4,2,32,384]{4,3,2,1,0:T(8,128)(2,1)S(1)}, bf16[4,4,2,32,384]{4,3,2,1,0:T(8,128)(2,1)S(1)}, u32[]{:S(2)}, u32[]{:S(2)}) collective-permute-start(bf16[4,4,2,32,384]{4,3,2,1,0:T(8,128)(2,1)S(1)} %shard_map.84.w0), channel_id=1, source_target_pairs={{0,6},{32,34},{2,4},{34,32},{4,2},{36,38},{6,0},{38,36},{1,7},{33,... | collective-permute-start | bytes 2359304 | tf_op jit(solution)/shard_map/ppermute | solution.py:40
  85.0 21.7 %collective-permute-start.7 = (bf16[4,2,32,384]{3,2,1,0:T(8,128)(2,1)S(1)}, bf16[4,2,32,384]{3,2,1,0:T(8,128)(2,1)S(1)}, u32[]{:S(2)}, u32[]{:S(2)}) collective-permute-start(bf16[4,2,32,384]{3,2,1,0:T(8,128)(2,1)S(1)} %collective-permute-done.5.p1), channel_id=1, source_target_pairs={{0,6},{32,34},{2,4},{34,32},{4,2},{36,38},{6,0},{38,36},{1,7},{33,... | collective-permute-start | bytes 589832 | tf_op jit(solution)/shard_map/ppermute | solution.py:40
  107.3 19.5 %collective-permute-start.8 = (bf16[4,4,2,32,384]{4,3,2,1,0:T(8,128)(2,1)S(1)}, bf16[4,4,2,32,384]{4,3,2,1,0:T(8,128)(2,1)S(1)}, u32[]{:S(2)}, u32[]{:S(2)}) collective-permute-start(bf16[4,4,2,32,384]{4,3,2,1,0:T(8,128)(2,1)S(1)} %shard_map.83.w0), channel_id=1, source_target_pairs={{0,64},{32,224},{64,0},{96,160},{128,192},{160,96},{192,128},{224,... | collective-permute-start | bytes 2359304 | tf_op jit(solution)/shard_map/ppermute | solution.py:40
  111.0 20.3 %collective-permute-start.25 = (bf16[2,4,4,32,512]{4,3,2,1,0:T(8,128)(2,1)S(1)}, bf16[2,4,4,32,512]{4,3,2,1,0:T(8,128)(2,1)S(1)}, u32[]{:S(2)}, u32[]{:S(2)}) collective-permute-start(bf16[2,4,4,32,512]{4,3,2,1,0:T(8,128)(2,1)S(1)} %collective-permute-done.24.o2), channel_id=1, source_target_pairs={{0,25},{32,40},{8,16},{40,32},{16,8},{48,56},{24,1},{56,48},{1,24}... | collective-permute-start | bytes 3145736 | tf_op jit(solution)/shard_map/ppermute | solution.py:40
  111.1 17.5 %collective-permute-start.15 = (bf16[4,4,2,32,384]{4,3,2,1,0:T(8,128)(2,1)S(1)}, bf16[4,4,2,32,384]{4,3,2,1,0:T(8,128)(2,1)S(1)}, u32[]{:S(2)}, u32[]{:S(2)}) collective-permute-start(bf16[4,4,2,32,384]{4,3,2,1,0:T(8,128)(2,1)S(1)} %shard_map.83.w0), channel_id=1, source_target_pairs={{0,192},{32,96},{64,128},{96,32},{128,64},{160,224},{192,0},{224,1... | collective-permute-start | bytes 2359304 | tf_op jit(solution)/shard_map/ppermute | solution.py:40
  111.1 19.7 %collective-permute-start.14 = (bf16[4,4,2,32,384]{4,3,2,1,0:T(8,128)(2,1)S(1)}, bf16[4,4,2,32,384]{4,3,2,1,0:T(8,128)(2,1)S(1)}, u32[]{:S(2)}, u32[]{:S(2)}) collective-permute-start(bf16[4,4,2,32,384]{4,3,2,1,0:T(8,128)(2,1)S(1)} %collective-permute-done.13.w1), channel_id=1, source_target_pairs={{0,6},{32,34},{2,4},{34,32},{4,2},{36,38},{6,0},{38,36},{1,7},{33,... | collective-permute-start | bytes 2359304 | tf_op jit(solution)/shard_map/ppermute | solution.py:40
  126.8 14.2 %collective-permute-start.9 = (bf16[4,4,2,32,384]{4,3,2,1,0:T(8,128)(2,1)S(1)}, bf16[4,4,2,32,384]{4,3,2,1,0:T(8,128)(2,1)S(1)}, u32[]{:S(2)}, u32[]{:S(2)}) collective-permute-start(bf16[4,4,2,32,384]{4,3,2,1,0:T(8,128)(2,1)S(1)} %collective-permute-done.8.w1), channel_id=1, source_target_pairs={{0,192},{32,96},{64,128},{96,32},{128,64},{160,224},{192,0},{224,1... | collective-permute-start | bytes 2359304 | tf_op jit(solution)/shard_map/ppermute | solution.py:40
  128.6 18.6 %collective-permute-start.26 = (bf16[2,4,4,32,512]{4,3,2,1,0:T(8,128)(2,1)S(1)}, bf16[2,4,4,32,512]{4,3,2,1,0:T(8,128)(2,1)S(1)}, u32[]{:S(2)}, u32[]{:S(2)}) collective-permute-start(bf16[2,4,4,32,512]{4,3,2,1,0:T(8,128)(2,1)S(1)} %maximum_select_fusion.o0), channel_id=1, source_target_pairs={{0,32},{32,0},{1,33},{33,1},{2,34},{34,2},{3,35},{35,3},{4,36},{36... | collective-permute-start | bytes 3145736 | tf_op jit(solution)/shard_map/ppermute | solution.py:336
  130.8 16.4 %collective-permute-start.27 = (bf16[2,4,4,32,512]{4,3,2,1,0:T(8,128)(2,1)S(1)}, bf16[2,4,4,32,512]{4,3,2,1,0:T(8,128)(2,1)S(1)}, u32[]{:S(2)}, u32[]{:S(2)}) collective-permute-start(bf16[2,4,4,32,512]{4,3,2,1,0:T(8,128)(2,1)S(1)} %collective-permute-done.23.o1), channel_id=1, source_target_pairs={{0,32},{32,0},{1,33},{33,1},{2,34},{34,2},{3,35},{35,3},{4,36},{36... | collective-permute-start | bytes 3145736 | tf_op jit(solution)/shard_map/ppermute | solution.py:336
  130.9 16.4 %collective-permute-start.28 = (bf16[2,4,4,32,512]{4,3,2,1,0:T(8,128)(2,1)S(1)}, bf16[2,4,4,32,512]{4,3,2,1,0:T(8,128)(2,1)S(1)}, u32[]{:S(2)}, u32[]{:S(2)}) collective-permute-start(bf16[2,4,4,32,512]{4,3,2,1,0:T(8,128)(2,1)S(1)} %collective-permute-done.24.o2), channel_id=1, source_target_pairs={{0,32},{32,0},{1,33},{33,1},{2,34},{34,2},{3,35},{35,3},{4,36},{36... | collective-permute-start | bytes 3145736 | tf_op jit(solution)/shard_map/ppermute | solution.py:336
  131.3 15.9 %collective-permute-start.29 = (bf16[2,4,4,32,512]{4,3,2,1,0:T(8,128)(2,1)S(1)}, bf16[2,4,4,32,512]{4,3,2,1,0:T(8,128)(2,1)S(1)}, u32[]{:S(2)}, u32[]{:S(2)}) collective-permute-start(bf16[2,4,4,32,512]{4,3,2,1,0:T(8,128)(2,1)S(1)} %collective-permute-done.25.o3), channel_id=1, source_target_pairs={{0,32},{32,0},{1,33},{33,1},{2,34},{34,2},{3,35},{35,3},{4,36},{36... | collective-permute-start | bytes 3145736 | tf_op jit(solution)/shard_map/ppermute | solution.py:336
  (10 other events, 107.6 us)
